TPU v7x, 32 devices: a whole 2x2x4 slice. The times are simulated.
32 devices in a mesh: copy: 2 (over core), fsdp: 4 (over z), tp: 4 (over y, x).
Axes of the slice: x: 2, y: 2, z: 4, core: 2. Of those that a mesh axis runs over, the one named last changes fastest.
Arguments:
- gradients: float32 [32, 128, 4096], P('copy', 'fsdp', 'tp'), parts along dimension 0, may hold values from -6 to 6
- momentum: float32 [32, 128, 4096], P('copy', 'fsdp', 'tp'), parts along dimension 0, may hold values from -6 to 6
- weights: float32 [32, 128, 4096], P('copy', 'fsdp', 'tp'), parts along dimension 0, may hold values from -0.1875 to 0.1875
Outputs:
- new_weights: float32 [32, 128, 4096], P('copy', 'fsdp', 'tp'), parts along dimension 0
- new_momentum: float32 [32, 128, 4096], P('copy', 'fsdp', 'tp'), parts along dimension 0
There are 2 independent parts, one for each index of `copy`. A program takes and returns all parts, laid end to end along the dimension named above; each array names one. Nothing has to cross between parts.
All inputs are finite; a program needn't handle non-finite values.
Results may differ from a plain program's by a relative error of at most 0.00014.
Values sent between devices are 32-bit elements; how exact they have to be, the bound alone decides.
A program may use at most 64 MiB of HBM per device.

v0:
```python
import jax
import jax.numpy as jnp
from jax import lax
from jax.sharding import PartitionSpec as P

ITERS = 4
hold_rate = 0.95
learn_rate = 0.9
decay_rate = 0.1


def mul(a, b):
    return jnp.einsum("mij,mjk->mik", a, b, precision=lax.Precision.HIGHEST)


def mixing(gram):
    eye = jnp.eye(gram.shape[-1], dtype=gram.dtype)
    scale = lax.rsqrt(jnp.sum(gram * eye, axis=(1, 2), keepdims=True) + 1e-06)
    gram = gram * scale * scale
    total = scale * eye
    for step in range(ITERS):
        poly = 3.4445 * eye - 4.775 * gram + 2.0315 * mul(gram, gram)
        total = mul(poly, total)
        if step < ITERS - 1:
            gram = mul(poly, mul(gram, poly))
    return total


def shards(gradients, momentum, weights):
    new_momentum = hold_rate * momentum + gradients
    direction = hold_rate * new_momentum + gradients
    moved = lax.all_to_all(direction, "fsdp", split_axis=0, concat_axis=1, tiled=True)
    gram = jnp.einsum("mik,mjk->mij", moved, moved, precision=lax.Precision.HIGHEST)
    gram = lax.psum(gram, "tp")
    iterate = mul(mixing(gram), moved)
    back = lax.all_to_all(iterate, "fsdp", split_axis=1, concat_axis=0, tiled=True)
    new_weights = (1.0 - learn_rate * decay_rate) * weights - learn_rate * back
    return (new_weights, new_momentum)


def solution(mesh):
    return jax.shard_map(
        shards,
        mesh=mesh,
        in_specs=(P("copy", "fsdp", "tp"), P("copy", "fsdp", "tp"), P("copy", "fsdp", "tp")),
        out_specs=(P("copy", "fsdp", "tp"), P("copy", "fsdp", "tp")),
        check_vma=False,
    )
```

profile of v0, /device:TPU:0, one launch (start us, length us, event | category | flops | bytes accessed | tf_op | source)
XLA Modules:
  0.0 186.5 jit_solution(14155956798188366832)
XLA Ops:
  7.2 4.5 %multiply_add_fusion = (f32[16,32,1024]{2,1,0:T(8,128)S(1)}, f32[16,32,1024]{2,1,0:T(8,128)}) fusion(f32[16,32,1024]{2,1,0:T(8,128)} %param.3, f32[16,32,1024]{2,1,0:T(8,128)} %param.4), kind=kLoop, calls=%fused_computation.1 | loop fusion | flops 2097152 | bytes 8388608 | tf_op jit(solution)/shard_map/add | solution.py:31
  11.7 54.3 %all_to_all.27 = f32[16,32,1024]{2,1,0:T(8,128)S(1)} all-to-all(f32[16,32,1024]{2,1,0:T(8,128)S(1)} %get-tuple-element.2), channel_id=1, replica_groups=mesh['copy'=2,'fsdp'=4,'tp'=4] {'fsdp'}, dimensions={0} | all-to-all | bytes 4194304 | tf_op jit(solution)/shard_map/all_to_all | solution.py:32
  66.2 2.8 %fusion.13 = f32[4,128,128]{2,1,0:T(8,128)} fusion(f32[4,128,1024]{2,1,0:T(8,128)S(1)} %bitcast.37), kind=kOutput, calls=%fused_computation.25 | convolution fusion | flops 805306368 | bytes 2359296 | tf_op jit(solution)/shard_map/mik,mjk->mij/dot_general | solution.py:33
  69.0 42.4 %all-reduce.2.cloned.1.call-done = f32[4,128,128]{2,1,0:T(8,128)} async-done(((f32[4,128,128]{2,1,0:T(8,128)}), f32[4,128,128]{2,1,0:T(8,128)}) %all-reduce.2.cloned.1.call-update) | async-done | bytes 262160 | tf_op jit(solution)/shard_map/psum | solution.py:34
  111.4 1.1 multiply_reduce_fusion
  112.5 1.6 fusion.3
  114.1 0.4 fusion.4
  114.6 1.4 fusion.6
  116.0 0.4 fusion.14
  116.4 0.4 fusion.2
  116.7 0.4 fusion.15
  117.1 0.4 fusion.19
  117.5 0.4 fusion.16
  118.0 0.4 fusion.1
  118.3 0.4 fusion.17
  118.7 0.4 fusion.20
  119.1 0.4 fusion.18
  119.9 0.4 fusion.21
  120.3 1.9 %fusion.22 = f32[4,128,1024]{2,1,0:T(8,128)S(1)} fusion(f32[4,128,128]{2,1,0:T(8,128)S(1)} %fusion.21, f32[4,128,1024]{2,1,0:T(8,128)S(1)} %bitcast.38), kind=kOutput, calls=%fused_computation.34 | convolution fusion | flops 805306368 | bytes 4456448 | tf_op jit(solution)/shard_map/mij,mjk->mik/dot_general | solution.py:13
  122.3 1.4 copy.8
  123.6 52.1 %all_to_all.28 = f32[4,128,1024]{2,0,1:T(4,128)S(1)} all-to-all(f32[4,128,1024]{2,0,1:T(4,128)S(1)} %copy.8), channel_id=1, replica_groups=mesh['copy'=2,'fsdp'=4,'tp'=4] {'fsdp'}, dimensions={1} | all-to-all | bytes 4194304 | tf_op jit(solution)/shard_map/all_to_all | solution.py:36
  175.7 0.6 broadcast_multiply_fusion
  176.3 1.2 copy.9
  177.9 1.8 bitcast_subtract_fusion
  (9 shorter events, 1.0 us)
Async XLA Ops:
  7.2 104.2 %all-reduce.2.cloned.1.call-start = ((), (), s32[]{:S(2)}) async-start(), calls=%async_computation.2 | async-start | bytes 524288 | tf_op jit(solution)/shard_map/psum | solution.py:34
  176.3 1.6 copy-start
Sparse Core Ops, SparseCore 0:
  69.1 42.2 all-reduce.1
where the time goes:
time: 187 us
  blocking collectives  106 us (57%)
  waiting for transfers between devices  42.4 us (23%)
  between operations  14.2 us (8%)
  matrix products  12.4 us (7%)
  other arithmetic  7.95 us (4%)
  local copies, waits for them, and re-layouts  3.07 us (2%)
    all_to_all x1, blocking collectives, shards(): lax.all_to_all(direction, 'fsdp', split_axis=0, concat_axis=1, tiled=True)  54.3 us
    all_to_all x1, blocking collectives, shards(): lax.all_to_all(iterate, 'fsdp', split_axis=1, concat_axis=0, tiled=True)  52.1 us
    psum x1, waiting for transfers between devices, shards(): gram = lax.psum(gram, 'tp')  42.4 us
    dot_general x15, matrix products, mul(): return jnp.einsum('mij,mjk->mik', a, b, precision=lax.Precision.HIGHEST)  9.65 us
    add x1, other arithmetic, shards(): direction = hold_rate * new_momentum + gradients  4.5 us
  transfers between devices with their start and end apart: 1, of which 1 were waited for; matrix products, arithmetic and copies ran while one was open for 0% of the time, Pallas kernels for 0%

commit v1 on v0

--- a/solution.py
+++ b/solution.py
@@ -31,7 +31,11 @@
     direction = hold_rate * new_momentum + gradients
     moved = lax.all_to_all(direction, "fsdp", split_axis=0, concat_axis=1, tiled=True)
     gram = jnp.einsum("mik,mjk->mij", moved, moved, precision=lax.Precision.HIGHEST)
-    gram = lax.psum(gram, "tp")
+
+    def _mix_quarters(local_block):
+        return jnp.sum(lax.all_gather(local_block, axis_name="tp"), axis=0)
+
+    gram = _mix_quarters(gram)
     iterate = mul(mixing(gram), moved)
     back = lax.all_to_all(iterate, "fsdp", split_axis=1, concat_axis=0, tiled=True)
     new_weights = (1.0 - learn_rate * decay_rate) * weights - learn_rate * back

time: 187 us -> 169 us (0.904)
  waiting for transfers between devices: 42.4 us -> 25.9 us
  matrix products: 12.4 us -> 10.3 us
    psum x1 -> x0, waiting for transfers between devices: 42.4 us -> none  [shards(): gram = lax.psum(gram, 'tp')]
    all_gather x0 -> x1, waiting for transfers between devices: none -> 25.9 us  [_mix_quarters(): return jnp.sum(lax.all_gather(local_block, axis_name='tp'), axis=0)]
    dot_general x15, matrix products: 9.65 us -> 7.57 us  [mul(): return jnp.einsum('mij,mjk->mik', a, b, precision=lax.Precision.HIGHEST)]
where the time goes in v1:
time: 169 us
  blocking collectives  107 us (63%)
  waiting for transfers between devices  25.9 us (15%)
  between operations  14.2 us (8%)
  matrix products  10.3 us (6%)
  other arithmetic  8.18 us (5%)
  local copies, waits for them, and re-layouts  3.17 us (2%)
    all_to_all x1, blocking collectives, shards(): lax.all_to_all(direction, 'fsdp', split_axis=0, concat_axis=1, tiled=True)  54.3 us
    all_to_all x1, blocking collectives, shards(): lax.all_to_all(iterate, 'fsdp', split_axis=1, concat_axis=0, tiled=True)  52.4 us
    all_gather x1, waiting for transfers between devices, _mix_quarters(): return jnp.sum(lax.all_gather(local_block, axis_name='tp'), axis=0)  25.9 us
    dot_general x15, matrix products, mul(): return jnp.einsum('mij,mjk->mik', a, b, precision=lax.Precision.HIGHEST)  7.57 us
    add x1, other arithmetic, shards(): direction = hold_rate * new_momentum + gradients  4.27 us
  transfers between devices with their start and end apart: 1, of which 1 were waited for; matrix products, arithmetic and copies ran while one was open for 0% of the time, Pallas kernels for 0%

profile of v1, /device:TPU:0, one launch (start us, length us, event | category | flops | bytes accessed | tf_op | source)
XLA Modules:
  0.0 168.5 jit_solution(15080903002159324298)
XLA Ops:
  7.2 4.3 %multiply_add_fusion = (f32[16,32,1024]{2,1,0:T(8,128)S(1)}, f32[16,32,1024]{2,1,0:T(8,128)}) fusion(f32[16,32,1024]{2,1,0:T(8,128)} %param.3, f32[16,32,1024]{2,1,0:T(8,128)} %param.4), kind=kLoop, calls=%fused_computation.1 | loop fusion | flops 2097152 | bytes 8388608 | tf_op jit(solution)/shard_map/add | solution.py:31
  11.5 54.3 %all_to_all.27 = f32[16,32,1024]{2,1,0:T(8,128)S(1)} all-to-all(f32[16,32,1024]{2,1,0:T(8,128)S(1)} %get-tuple-element.2), channel_id=1, replica_groups=mesh['copy'=2,'fsdp'=4,'tp'=4] {'fsdp'}, dimensions={0} | all-to-all | bytes 4194304 | tf_op jit(solution)/shard_map/all_to_all | solution.py:32
  66.1 2.8 %fusion.13 = f32[4,128,128]{2,1,0:T(8,128)} fusion(f32[4,128,1024]{2,1,0:T(8,128)S(1)} %bitcast.38), kind=kOutput, calls=%fused_computation.25 | convolution fusion | flops 805306368 | bytes 2359296 | tf_op jit(solution)/shard_map/mik,mjk->mij/dot_general | solution.py:33
  68.9 25.9 %all-gather.3.cloned.1.call-done = f32[16,128,128]{2,1,0:T(8,128)} async-done(((f32[4,128,128]{2,1,0:T(8,128)}), f32[16,128,128]{2,1,0:T(8,128)}) %all-gather.3.cloned.1.call-update) | async-done | bytes 1048592 | tf_op jit(solution)/shard_map/all_gather | solution.py:36
  94.7 1.3 reduce_sum.18
  96.2 0.5 fusion.3
  96.7 0.4 fusion.6
  97.1 0.4 fusion.4
  97.6 0.4 fusion.14
  98.0 0.4 fusion.2
  98.4 0.4 fusion.15
  98.8 0.4 fusion.19
  99.2 0.4 fusion.16
  99.6 0.4 fusion.1
  100.0 0.4 fusion.17
  100.4 0.4 fusion.20
  100.8 0.4 fusion.18
  101.5 0.4 fusion.21
  101.9 1.9 %fusion.22 = f32[4,128,1024]{2,1,0:T(8,128)S(1)} fusion(f32[4,128,128]{2,1,0:T(8,128)S(1)} %fusion.21, f32[4,128,1024]{2,1,0:T(8,128)S(1)} %bitcast.39), kind=kOutput, calls=%fused_computation.34 | convolution fusion | flops 805306368 | bytes 4456448 | tf_op jit(solution)/shard_map/mij,mjk->mik/dot_general | solution.py:13
  103.9 1.4 copy.8
  105.2 52.4 %all_to_all.28 = f32[4,128,1024]{2,0,1:T(4,128)S(1)} all-to-all(f32[4,128,1024]{2,0,1:T(4,128)S(1)} %copy.8), channel_id=1, replica_groups=mesh['copy'=2,'fsdp'=4,'tp'=4] {'fsdp'}, dimensions={1} | all-to-all | bytes 4194304 | tf_op jit(solution)/shard_map/all_to_all | solution.py:40
  157.7 0.7 broadcast_multiply_fusion
  158.4 1.2 copy.9
  159.9 1.8 %bitcast_subtract_fusion = f32[16,32,1024]{2,1,0:T(8,128)} fusion(f32[4,4,32,1024]{3,2,1,0:T(8,128)S(1)} %copy.9, f32[16,32,1024]{2,1,0:T(8,128)S(1)} %copy-done), kind=kLoop, calls=%fused_computation | loop fusion | flops 1048576 | bytes 6291456 | tf_op jit(solution)/shard_map/sub | solution.py:41
  (10 shorter events, 1.2 us)
Async XLA Ops:
  7.2 87.6 %all-gather.3.cloned.1.call-start = ((), (), s32[]{:S(2)}) async-start(), calls=%async_computation.2 | async-start | bytes 1310720 | tf_op jit(solution)/shard_map/all_gather | solution.py:36
  158.4 1.6 copy-start
Sparse Core Ops, SparseCore 0:
  69.0 25.7 all-gather.2
